TPU v7x, 32 devices: a whole 2x2x4 slice. The times are simulated.
32 devices in a mesh: mem: 8 (over z, x), chan: 4 (over y, core).
Axes of the slice: x: 2, y: 2, z: 4, core: 2. Of those that a mesh axis runs over, the one named last changes fastest.
Arguments:
- state_anom: bfloat16 [8, 64, 137], P(None, 'mem'), may hold values from -6 to 6
- radiance_anom: bfloat16 [8, 64, 8704], P(None, 'mem', 'chan'), may hold values from -6 to 6
- inv_noise: float32 [8704], P('chan'), may hold values from 0.02 to 0.2
- innovation: float32 [8, 8704], P(None, 'chan'), may hold values from -6 to 6
- valid_count: int32 [8], replicated, may hold values from 4352 to 8461
Outputs:
- information: float32 [8, 137, 137], P('mem')
- gradient: float32 [8, 137], P('mem')
- increment: float32 [8, 137], P('mem')
All inputs are finite; a program needn't handle non-finite values.
Results may differ from a plain program's by a relative error of at most 0.0003.
Values may be sent and summed in bfloat16 or wider, within the bound.
A program may use at most 64 MiB of HBM per device.

v0:
```python
import jax
import jax.numpy as jnp
from jax import lax
from jax.sharding import PartitionSpec as P


def slab_terms(cross, weight, innov_rows):
    weighted = cross * weight[:, :, None]
    info_part = jnp.einsum("pcs,pct->pst", weighted, cross, precision=lax.Precision.HIGHEST)
    grad_part = jnp.einsum("pcs,pc->ps", weighted, innov_rows, precision=lax.Precision.HIGHEST)
    return (info_part, grad_part)


def shards(state_anom, radiance_anom, inv_noise, innovation, valid_count):
    profiles = state_anom.shape[0]
    states = state_anom.shape[2]
    slab_width = radiance_anom.shape[2]
    members_all = state_anom.shape[1] * lax.axis_size("mem")
    prof_local = profiles // lax.axis_size("mem")
    slab_start = lax.axis_index("chan") * slab_width
    own_rad, own_states = (
        lax.all_to_all(radiance_anom, "mem", split_axis=0, concat_axis=1, tiled=True),
        lax.all_to_all(state_anom, "mem", split_axis=0, concat_axis=1, tiled=True),
    )
    cross = jnp.einsum("pmc,pms->pcs", own_rad, own_states, preferred_element_type=jnp.float32)
    cross = cross / jnp.float32(members_all - 1)
    first_prof = lax.axis_index("mem") * prof_local
    own_count = lax.dynamic_slice_in_dim(valid_count, first_prof, prof_local, 0)
    slots = slab_start + jnp.arange(slab_width, dtype=jnp.int32)
    valid = (slots[None, :] < own_count[:, None]).astype(jnp.float32)
    weight = inv_noise[None, :] * valid
    innov_rows = lax.dynamic_slice_in_dim(innovation, first_prof, prof_local, 0)
    info_share, grad_share = slab_terms(cross, weight, innov_rows)
    information, gradient = lax.psum((info_share, grad_share), "chan")
    system = information + jnp.eye(states, dtype=jnp.float32)[None]
    factor = jnp.linalg.cholesky(system)
    increment = jax.scipy.linalg.cho_solve((factor, True), gradient[:, :, None])[:, :, 0]
    return (information, gradient, increment)


def solution(mesh):
    in_specs = (P(None, "mem", None), P(None, "mem", "chan"), P("chan"), P(None, "chan"), P())
    out_specs = (P("mem", None, None), P("mem", None), P("mem", None))
    return jax.shard_map(shards, mesh=mesh, in_specs=in_specs, out_specs=out_specs, check_vma=False)
```

profile of v0, /device:TPU:0, one launch (start us, length us, event | category | flops | bytes accessed | tf_op | source)
XLA Modules:
  0.0 121.7 jit_solution(8152377795422508364)
XLA Ops:
  7.2 0.0 copy-start
  7.2 14.1 %all_to_all.8 = bf16[8,8,137]{2,1,0:T(8,128)(2,1)S(1)} all-to-all(bf16[8,8,137]{2,1,0:T(8,128)(2,1)} %param.5), channel_id=1, replica_groups=mesh['mem'=8,'chan'=4] {'mem'}, dimensions={0} | all-to-all | bytes 35072 | tf_op jit(solution)/shard_map/all_to_all | solution.py:23
  21.3 3.4 %all-to-all-start = ((bf16[8,8,2176]{2,1,0:T(8,128)(2,1)}), bf16[8,8,2176]{2,1,0:T(8,128)(2,1)S(1)}, u32[]{:S(2)}, u32[]{:S(2)}) async-start(bf16[8,8,2176]{2,1,0:T(8,128)(2,1)} %param.6), calls=%async_computation | async-start | bytes 557056 | tf_op jit(solution)/shard_map/all_to_all | solution.py:22
  24.7 0.0 all-reduce.5.cloned.1.call-start
  24.8 1.2 %dynamic_slice.6 = s32[1]{0:T(128)} dynamic-slice(s32[8]{0:T(128)} %param.9, s32[]{:T(128)S(6)} %select_n.8), dynamic_slice_sizes={1} | dynamic-slice | bytes 12 | tf_op jit(solution)/shard_map/dynamic_slice | solution.py:28
  26.1 1.4 %select_multiply_fusion = f32[2176]{0:T(1024)S(1)} fusion(f32[2176]{0:T(1024)} %param.7, s32[]{:T(128)} %bitcast.1, s32[]{:T(128)S(6)} %mul.19), kind=kLoop, calls=%fused_computation.43 | loop fusion | flops 8704 | bytes 17416 | tf_op jit(solution)/shard_map/mul | solution.py:8
  27.4 5.6 %all-to-all-done = bf16[8,8,2176]{2,1,0:T(8,128)(2,1)S(1)} async-done(((bf16[8,8,2176]{2,1,0:T(8,128)(2,1)}), bf16[8,8,2176]{2,1,0:T(8,128)(2,1)S(1)}, u32[]{:S(2)}, u32[]{:S(2)}) %all-to-all-start) | async-done | bytes 278560 | tf_op jit(solution)/shard_map/all_to_all | solution.py:22
  33.0 0.4 convolution_bitcast_fusion
  33.4 1.9 %fusion.5 = f32[1,137,137]{1,2,0:T(8,128)} fusion(f32[2176,137]{0,1:T(8,128)S(1)} %convolution_bitcast_fusion, f32[2176]{0:T(1024)S(1)} %select_multiply_fusion), kind=kOutput, calls=%fused_computation.6 | convolution fusion | flops 490692352 | bytes 1276228 | tf_op jit(solution)/shard_map/pcs,pct->pst/dot_general | solution.py:9
  35.3 0.0 all-reduce.5.cloned.1.call-update
  35.3 0.0 copy-done
  35.3 1.1 fusion.2
  36.5 5.8 %psum.15 = f32[1,137]{1,0:T(1,128)S(1)} all-reduce(f32[1,137]{1,0:T(1,128)S(1)} %fusion.2), channel_id=1, replica_groups=mesh['mem'=8,'chan'=4] {'chan'}, use_global_device_ids=true, to_apply=%region_1.0 | all-reduce | flops 137 | bytes 1096 | tf_op jit(solution)/shard_map/psum | solution.py:34
  42.3 0.0 copy-start.2
  42.3 23.1 %all-reduce.5.cloned.1.call-done = f32[1,137,137]{1,2,0:T(8,128)} async-done(((f32[1,137,137]{1,2,0:T(8,128)}), f32[1,137,137]{1,2,0:T(8,128)}) %all-reduce.5.cloned.1.call-update) | async-done | bytes 75092 | tf_op jit(solution)/shard_map/psum | solution.py:34
  65.4 0.9 convert_add_fusion
  66.3 0.0 copy-start.1
  66.3 0.1 copy.9
  66.4 0.9 fusion.18
  67.4 11.7 %custom-call.20 = f32[1,128,128]{2,1,0:T(8,128)S(1)} custom-call(f32[1,128,128]{2,1,0:T(8,128)S(1)} %cholesky.123), custom_call_target="Cholesky" | custom-call | tf_op jit(solution)/shard_map/jit(cholesky)/cholesky | solution.py:36
  79.2 9.8 %custom-call.21 = f32[1,1,128,128]{2,3,1,0:T(8,128)S(1)} custom-call(f32[1,1,128,128]{3,2,1,0:T(8,128)S(1)} %get-tuple-element.27), custom_call_target="InvertDiagBlocksLowerTriangular" | custom-call | tf_op jit(solution)/shard_map/jit(cholesky)/cholesky | solution.py:36
  89.0 0.2 bitcast_dynamic-update-slice_fusion
  89.1 0.1 fusion.10
  89.3 0.8 custom-call.22
  90.1 0.7 compare_reduce_fusion.1
  90.8 0.6 compare_reduce_fusion
  92.7 0.1 fusion.19
  92.9 19.7 %custom-call.23 = f32[2,128,128]{1,2,0:T(8,128)S(1)} custom-call(f32[2,128,128]{2,1,0:T(8,128)S(1)} %pad_maximum_fusion), custom_call_target="InvertDiagBlocksLowerTriangular" | custom-call | tf_op jit(solution)/shard_map/jit(_cho_solve)/triangular_solve | solution.py:37
  112.5 0.2 fusion.22
  112.7 0.0 copy-done.2
  112.7 0.1 fusion.14
  112.8 0.1 convolution_bitcast_fusion.5
  113.0 0.1 convolution_bitcast_fusion.4
  113.1 0.1 fusion.12
  113.3 0.2 convolution_bitcast_fusion.2
  113.5 0.6 maximum_bitcast_fusion
  114.1 0.0 copy-done.1
  114.1 0.8 copy.11
  (9 shorter events, 0.1 us)
Async XLA Ops:
  7.2 28.2 %copy-start = (f32[8,2176]{1,0:T(8,128)S(1)}, f32[8,2176]{1,0:T(8,128)}, u32[]{:S(2)}) copy-start(f32[8,2176]{1,0:T(8,128)} %param.8) | copy-start | bytes 208900
  21.3 11.7 %all-to-all-start = ((bf16[8,8,2176]{2,1,0:T(8,128)(2,1)}), bf16[8,8,2176]{2,1,0:T(8,128)(2,1)S(1)}, u32[]{:S(2)}, u32[]{:S(2)}) async-start(bf16[8,8,2176]{2,1,0:T(8,128)(2,1)} %param.6), calls=%async_computation | async-start | bytes 557056 | tf_op jit(solution)/shard_map/all_to_all | solution.py:22
  24.7 40.7 %all-reduce.5.cloned.1.call-start = ((), (), s32[]{:S(2)}) async-start(), calls=%async_computation.2 | async-start | bytes 294912 | tf_op jit(solution)/shard_map/psum | solution.py:34
  42.3 70.4 %copy-start.2 = (f32[1,137]{1,0:T(1,128)}, f32[1,137]{1,0:T(1,128)S(1)}, u32[]{:S(2)}) copy-start(f32[1,137]{1,0:T(1,128)S(1)} %psum.15) | copy-start | bytes 1648
  66.3 47.8 %copy-start.1 = (f32[1,137,137]{1,2,0:T(8,128)S(1)}, f32[1,137,137]{1,2,0:T(8,128)}, u32[]{:S(2)}) copy-start(f32[1,137,137]{1,2,0:T(8,128)} %all-reduce.5.cloned.1.call-done) | copy-start | bytes 225232
Sparse Core Ops, SparseCore 0:
  35.5 29.8 all-reduce.4
where the time goes:
time: 122 us
  other arithmetic  47.4 us (39%)
  waiting for transfers between devices  28.7 us (24%)
  blocking collectives  19.9 us (16%)
  between operations  15.5 us (13%)
  matrix products  4.67 us (4%)
  starting transfers between devices  3.46 us (3%)
  local copies, waits for them, and re-layouts  2.15 us (2%)
    another operation x7, other arithmetic, shards(): factor = jnp.linalg.cholesky(system)  23.7 us
    psum x1, waiting for transfers between devices, shards(): information, gradient = lax.psum((info_share, grad_share), 'chan')  23.1 us
    another operation x6, other arithmetic, shards(): jax.scipy.linalg.cho_solve((factor, True), gradient[:, :, None])[:, :, 0]  19.8 us
    all_to_all x1, blocking collectives, shards(): lax.all_to_all(state_anom, 'mem', split_axis=0, concat_axis=1, tiled=True)  14.1 us
    psum x1, blocking collectives, shards(): information, gradient = lax.psum((info_share, grad_share), 'chan')  5.84 us
    all_to_all x1, waiting for transfers between devices, shards(): lax.all_to_all(radiance_anom, 'mem', split_axis=0, concat_axis=1, tiled=T...  5.57 us
    all_to_all x1, starting transfers between devices, shards(): lax.all_to_all(radiance_anom, 'mem', split_axis=0, concat_axis=1, tiled=T...  3.42 us
  transfers between devices with their start and end apart: 2, of which 2 were waited for; matrix products, arithmetic and copies ran while one was open for 3% of the time, Pallas kernels for 0%

commit v1 on v0

--- a/solution.py
+++ b/solution.py
@@ -19,7 +19,12 @@
     prof_local = profiles // lax.axis_size("mem")
     slab_start = lax.axis_index("chan") * slab_width
     own_rad, own_states = (
-        lax.all_to_all(radiance_anom, "mem", split_axis=0, concat_axis=1, tiled=True),
+        jnp.concatenate(
+            lax.all_to_all(
+                jnp.stack(jnp.split(radiance_anom, lax.axis_size("mem"), axis=0)), "mem", 0, 0
+            ),
+            axis=1,
+        ),
         lax.all_to_all(state_anom, "mem", split_axis=0, concat_axis=1, tiled=True),
     )
     cross = jnp.einsum("pmc,pms->pcs", own_rad, own_states, preferred_element_type=jnp.float32)

time: 122 us -> 130 us (1.066)
  blocking collectives: 19.9 us -> 5.87 us
  local copies, waits for them, and re-layouts: 2.15 us -> 13.2 us
  starting transfers between devices: 3.46 us -> 13.5 us
  waiting for transfers between devices: 28.7 us -> 30 us
    all_to_all x1 -> x0, blocking collectives: 14.1 us -> none  [shards(): lax.all_to_all(state_anom, 'mem', split_axis=0, concat_axis=1, tiled=True)]
    all_to_all x1 -> x2, starting transfers between devices: 3.42 us -> 13.4 us  [the longest x1 7.42 us: shards(): lax.all_to_all(state_anom, 'mem', split_axis=0, concat_axis=1, tiled=True)]
    unnamed x7 -> x16, local copies, waits for them, and re-layouts: 0.79 us -> 10.4 us
    another operation x0 -> x1, local copies, waits for them, and re-layouts: none -> 1.38 us  [shards(): jnp.stack(jnp.split(radiance_anom, lax.axis_size('mem'), axis=0))]
    all_to_all x1 -> x2, waiting for transfers between devices: 5.57 us -> 6.77 us  [the longest x1 6.76 us: shards(): lax.all_to_all(jnp.stack(jnp.split(radiance_anom, lax.axis_size('mem'), a...]
  transfers between devices with their start and end apart: 2 -> 3, of which waited for: 2 -> 2; matrix products, arithmetic and copies ran while one was open for 3% -> 11% of each run, Pallas kernels for 0% -> 0%
where the time goes in v1:
time: 130 us; the launch traced here: 129 us
  other arithmetic  46.6 us (36%)
  waiting for transfers between devices  30 us (23%)
  between operations  15.5 us (12%)
  starting transfers between devices  13.5 us (10%)
  local copies, waits for them, and re-layouts  13.2 us (10%)
  blocking collectives  5.87 us (5%)
  matrix products  4.66 us (4%)
    another operation x7, other arithmetic, shards(): factor = jnp.linalg.cholesky(system)  23.7 us
    psum x1, waiting for transfers between devices, shards(): information, gradient = lax.psum((info_share, grad_share), 'chan')  23.2 us
    another operation x6, other arithmetic, shards(): jax.scipy.linalg.cho_solve((factor, True), gradient[:, :, None])[:, :, 0]  19.8 us
    unnamed x16, local copies, waits for them, and re-layouts  10.4 us
    all_to_all x1, starting transfers between devices, shards(): lax.all_to_all(state_anom, 'mem', split_axis=0, concat_axis=1, tiled=True)  7.42 us
    all_to_all x1, waiting for transfers between devices, shards(): lax.all_to_all(jnp.stack(jnp.split(radiance_anom, lax.axis_size('mem'), a...  6.76 us
    all_to_all x1, starting transfers between devices, shards(): lax.all_to_all(jnp.stack(jnp.split(radiance_anom, lax.axis_size('mem'), a...  6 us
    psum x1, blocking collectives, shards(): information, gradient = lax.psum((info_share, grad_share), 'chan')  5.87 us
  transfers between devices with their start and end apart: 3, of which 2 were waited for; matrix products, arithmetic and copies ran while one was open for 11% of the time, Pallas kernels for 0%

profile of v1, /device:TPU:0, one launch (start us, length us, event | category | flops | bytes accessed | tf_op | source)
XLA Modules:
  0.0 129.3 jit_solution(3980842012712749811)
XLA Ops:
  7.2 0.0 copy-start
  7.2 0.0 copy-start.2
  7.2 7.4 %all-to-all-start.1 = ((bf16[8,8,137]{2,1,0:T(8,128)(2,1)}), bf16[8,8,137]{2,1,0:T(8,128)(2,1)S(1)}, u32[]{:S(2)}, u32[]{:S(2)}) async-start(bf16[8,8,137]{2,1,0:T(8,128)(2,1)} %param.5), calls=%async_computation.1 | async-start | bytes 65536 | tf_op jit(solution)/shard_map/all_to_all | solution.py:28
  14.6 1.4 %bitcast_dynamic-update-slice_fusion.7 = bf16[8,1,8,2176]{3,2,1,0:T(8,128)(2,1)} fusion(bf16[8,8,2176]{2,1,0:T(8,128)(2,1)} %param.6), kind=kLoop, calls=%fused_computation.51 | loop fusion | bytes 69632
  16.0 1.4 %bitcast_dynamic-update-slice_fusion.6 = bf16[8,1,8,2176]{3,2,1,0:T(8,128)(2,1)} fusion(bf16[8,1,8,2176]{3,2,1,0:T(8,128)(2,1)} %bitcast_dynamic-update-slice_fusion.7, bf16[8,8,2176]{2,1,0:T(8,128)(2,1)} %param.6), kind=kLoop, calls=%fused_computation.50 | loop fusion | bytes 69632
  17.4 1.4 %bitcast_dynamic-update-slice_fusion.5 = bf16[8,1,8,2176]{3,2,1,0:T(8,128)(2,1)} fusion(bf16[8,1,8,2176]{3,2,1,0:T(8,128)(2,1)} %bitcast_dynamic-update-slice_fusion.6, bf16[8,8,2176]{2,1,0:T(8,128)(2,1)} %param.6), kind=kLoop, calls=%fused_computation.49 | loop fusion | bytes 69632
  18.7 1.4 %bitcast_dynamic-update-slice_fusion.4 = bf16[8,1,8,2176]{3,2,1,0:T(8,128)(2,1)} fusion(bf16[8,1,8,2176]{3,2,1,0:T(8,128)(2,1)} %bitcast_dynamic-update-slice_fusion.5, bf16[8,8,2176]{2,1,0:T(8,128)(2,1)} %param.6), kind=kLoop, calls=%fused_computation.48 | loop fusion | bytes 69632
  20.1 1.4 %bitcast_dynamic-update-slice_fusion.3 = bf16[8,1,8,2176]{3,2,1,0:T(8,128)(2,1)} fusion(bf16[8,1,8,2176]{3,2,1,0:T(8,128)(2,1)} %bitcast_dynamic-update-slice_fusion.4, bf16[8,8,2176]{2,1,0:T(8,128)(2,1)} %param.6), kind=kLoop, calls=%fused_computation.47 | loop fusion | bytes 69632
  21.5 1.4 %bitcast_dynamic-update-slice_fusion.2 = bf16[8,1,8,2176]{3,2,1,0:T(8,128)(2,1)} fusion(bf16[8,1,8,2176]{3,2,1,0:T(8,128)(2,1)} %bitcast_dynamic-update-slice_fusion.3, bf16[8,8,2176]{2,1,0:T(8,128)(2,1)} %param.6), kind=kLoop, calls=%fused_computation.46 | loop fusion | bytes 69632
  22.9 1.4 %bitcast_dynamic-update-slice_fusion.1 = bf16[8,1,8,2176]{3,2,1,0:T(8,128)(2,1)} fusion(bf16[8,1,8,2176]{3,2,1,0:T(8,128)(2,1)} %bitcast_dynamic-update-slice_fusion.2, bf16[8,8,2176]{2,1,0:T(8,128)(2,1)} %param.6), kind=kLoop, calls=%fused_computation.45 | loop fusion | bytes 69632
  24.2 1.4 %bitcast_dynamic-update-slice_fusion = bf16[8,1,8,2176]{3,2,1,0:T(8,128)(2,1)} fusion(bf16[8,1,8,2176]{3,2,1,0:T(8,128)(2,1)} %bitcast_dynamic-update-slice_fusion.1, bf16[8,8,2176]{2,1,0:T(8,128)(2,1)} %param.6), kind=kLoop, calls=%fused_computation.44 | loop fusion | bytes 69632 | tf_op jit(solution)/shard_map/stack | solution.py:24
  25.6 0.0 all-to-all-done.1
  25.6 6.0 %all-to-all-start = ((bf16[8,1,8,2176]{3,2,1,0:T(8,128)(2,1)}), bf16[8,1,8,2176]{3,2,1,0:T(8,128)(2,1)S(1)}, u32[]{:S(2)}, u32[]{:S(2)}) async-start(bf16[8,1,8,2176]{3,2,1,0:T(8,128)(2,1)} %bitcast_dynamic-update-slice_fusion), calls=%async_computation | async-start | bytes 557056 | tf_op jit(solution)/shard_map/all_to_all | solution.py:23
  31.6 0.0 all-reduce.5.cloned.1.call-start
  31.7 1.2 dynamic_slice.6
  33.0 0.0 copy-done.2
  33.0 0.7 select_multiply_fusion
  33.6 6.8 %all-to-all-done = bf16[8,1,8,2176]{3,2,1,0:T(8,128)(2,1)S(1)} async-done(((bf16[8,1,8,2176]{3,2,1,0:T(8,128)(2,1)}), bf16[8,1,8,2176]{3,2,1,0:T(8,128)(2,1)S(1)}, u32[]{:S(2)}, u32[]{:S(2)}) %all-to-all-start) | async-done | bytes 278560 | tf_op jit(solution)/shard_map/all_to_all | solution.py:23
  40.4 0.4 fusion.18
  40.8 1.9 %fusion.5 = f32[1,137,137]{1,2,0:T(8,128)} fusion(f32[2176,137]{0,1:T(8,128)S(1)} %fusion.18, f32[2176]{0:T(1024)S(1)} %select_multiply_fusion), kind=kOutput, calls=%fused_computation.5 | convolution fusion | flops 490692352 | bytes 1276228 | tf_op jit(solution)/shard_map/pcs,pct->pst/dot_general | solution.py:9
  42.7 0.0 all-reduce.5.cloned.1.call-update
  42.7 0.0 copy-done
  42.7 1.1 fusion.2
  43.9 5.9 %psum.15 = f32[1,137]{1,0:T(1,128)S(1)} all-reduce(f32[1,137]{1,0:T(1,128)S(1)} %fusion.2), channel_id=1, replica_groups=mesh['mem'=8,'chan'=4] {'chan'}, use_global_device_ids=true, to_apply=%region_1.0 | all-reduce | flops 137 | bytes 1096 | tf_op jit(solution)/shard_map/psum | solution.py:39
  49.8 23.2 %all-reduce.5.cloned.1.call-done = f32[1,137,137]{1,2,0:T(8,128)} async-done(((f32[1,137,137]{1,2,0:T(8,128)}), f32[1,137,137]{1,2,0:T(8,128)}) %all-reduce.5.cloned.1.call-update) | async-done | bytes 75092 | tf_op jit(solution)/shard_map/psum | solution.py:39
  73.0 0.9 convert_add_fusion
  73.9 0.0 copy-start.1
  73.9 0.1 copy.9
  74.0 0.9 fusion.20
  75.0 11.7 %custom-call.20 = f32[1,128,128]{2,1,0:T(8,128)S(1)} custom-call(f32[1,128,128]{2,1,0:T(8,128)S(1)} %cholesky.123), custom_call_target="Cholesky" | custom-call | tf_op jit(solution)/shard_map/jit(cholesky)/cholesky | solution.py:41
  86.8 9.8 %custom-call.21 = f32[1,1,128,128]{2,3,1,0:T(8,128)S(1)} custom-call(f32[1,1,128,128]{3,2,1,0:T(8,128)S(1)} %get-tuple-element.27), custom_call_target="InvertDiagBlocksLowerTriangular" | custom-call | tf_op jit(solution)/shard_map/jit(cholesky)/cholesky | solution.py:41
  96.6 0.2 bitcast_dynamic-update-slice_fusion.8
  96.7 0.1 fusion.10
  96.9 0.8 custom-call.22
  97.6 0.7 compare_reduce_fusion.1
  98.4 0.6 compare_reduce_fusion
  100.3 0.1 fusion.21
  100.4 19.7 %custom-call.23 = f32[2,128,128]{1,2,0:T(8,128)S(1)} custom-call(f32[2,128,128]{2,1,0:T(8,128)S(1)} %pad_maximum_fusion), custom_call_target="InvertDiagBlocksLowerTriangular" | custom-call | tf_op jit(solution)/shard_map/jit(_cho_solve)/triangular_solve | solution.py:42
  120.1 0.2 fusion.24
  120.3 0.0 copy-done.3
  120.3 0.1 fusion.14
  120.4 0.1 convolution_bitcast_fusion.4
  120.6 0.1 convolution_bitcast_fusion.3
  120.7 0.1 fusion.12
  120.9 0.2 convolution_bitcast_fusion.1
  121.0 0.6 maximum_bitcast_fusion
  121.7 0.0 copy-done.1
  121.7 0.8 copy.11
  (10 shorter events, 0.1 us)
Async XLA Ops:
  7.2 35.6 %copy-start = (f32[8,2176]{1,0:T(8,128)S(1)}, f32[8,2176]{1,0:T(8,128)}, u32[]{:S(2)}) copy-start(f32[8,2176]{1,0:T(8,128)} %param.8) | copy-start | bytes 208900
  7.2 25.8 %copy-start.2 = (f32[2176]{0:T(1024)S(1)}, f32[2176]{0:T(1024)}, u32[]{:S(2)}) copy-start(f32[2176]{0:T(1024)} %param.7) | copy-start | bytes 26116
  7.2 18.4 %all-to-all-start.1 = ((bf16[8,8,137]{2,1,0:T(8,128)(2,1)}), bf16[8,8,137]{2,1,0:T(8,128)(2,1)S(1)}, u32[]{:S(2)}, u32[]{:S(2)}) async-start(bf16[8,8,137]{2,1,0:T(8,128)(2,1)} %param.5), calls=%async_computation.1 | async-start | bytes 65536 | tf_op jit(solution)/shard_map/all_to_all | solution.py:28
  25.6 14.8 %all-to-all-start = ((bf16[8,1,8,2176]{3,2,1,0:T(8,128)(2,1)}), bf16[8,1,8,2176]{3,2,1,0:T(8,128)(2,1)S(1)}, u32[]{:S(2)}, u32[]{:S(2)}) async-start(bf16[8,1,8,2176]{3,2,1,0:T(8,128)(2,1)} %bitcast_dynamic-update-slice_fusion), calls=%async_computation | async-start | bytes 557056 | tf_op jit(solution)/shard_map/all_to_all | solution.py:23
  31.6 41.4 %all-reduce.5.cloned.1.call-start = ((), (), s32[]{:S(2)}) async-start(), calls=%async_computation.2 | async-start | bytes 294912 | tf_op jit(solution)/shard_map/psum | solution.py:39
  49.8 70.5 %copy-start.3 = (f32[1,137]{1,0:T(1,128)}, f32[1,137]{1,0:T(1,128)S(1)}, u32[]{:S(2)}) copy-start(f32[1,137]{1,0:T(1,128)S(1)} %psum.15) | copy-start | bytes 1648
  73.9 47.8 %copy-start.1 = (f32[1,137,137]{1,2,0:T(8,128)S(1)}, f32[1,137,137]{1,2,0:T(8,128)}, u32[]{:S(2)}) copy-start(f32[1,137,137]{1,2,0:T(8,128)} %all-reduce.5.cloned.1.call-done) | copy-start | bytes 225232
Sparse Core Ops, SparseCore 0:
  42.9 30.0 all-reduce.4
